TPU v7x, 32 devices: a whole 2x2x4 slice. The times are simulated.
32 devices in a mesh: grp: 4 (over y, x), row: 8 (over z, core).
Axes of the slice: x: 2, y: 2, z: 4, core: 2. Of those that a mesh axis runs over, the one named last changes fastest.
Arguments:
- blocks: bfloat16 [32, 4, 10, 256, 256], P(('grp', 'row')), may hold values from 0 to 1
- columns: int32 [32, 4, 10], P(('grp', 'row')), may hold values from -1 to 31, as said below
- factor: bfloat16 [64, 8192], P(None, ('grp', 'row')), may hold values from 0 to 0.3, as said below
Outputs:
- updated: float32 [64, 8192], P(None, ('grp', 'row'))
Inputs may be any that keep to these rules, and one draw needn't show every extreme that they name: Tile row i lies in group g = i // 8. In block h of tile row i the live slots come first and name distinct tile columns of group h (h * 8 to h * 8 + 7), none above i; block g always names i itself; blocks h > g are empty; a block holds at most 10 live slots, and -1 marks an empty slot. `factor`: entries are nonnegative.
All inputs are finite; a program needn't handle non-finite values.
Results may differ from a plain program's by a relative error of at most 0.0003.
Values may be sent and summed in bfloat16 or wider, within the bound.
No kernel may reach another device: no remote copies, remote signals or barrier semaphores. Data moves between devices by JAX's collectives and lax.ppermute only.
A program may use at most 128 MiB of HBM per device.

v0:
```python
import functools

import jax
import jax.numpy as jnp
from jax import lax
from jax.experimental import pallas as pl
from jax.experimental.pallas import tpu as pltpu
from jax.sharding import PartitionSpec as P


floor_value = 1e-06
VMEM = pl.BlockSpec(memory_space=pltpu.VMEM)
SMEM = pl.BlockSpec(memory_space=pltpu.SMEM)
HBM = pl.BlockSpec(memory_space=pltpu.HBM)
f32 = jnp.float32
bf16 = jnp.bfloat16


def call(kernel, in_specs, out_shape, limit, flops, nbytes, scratch=()):
    return pl.pallas_call(
        kernel,
        in_specs=in_specs,
        out_specs=[VMEM] * len(out_shape),
        out_shape=out_shape,
        scratch_shapes=list(scratch),
        compiler_params=pltpu.CompilerParams(vmem_limit_bytes=limit),
        cost_estimate=pl.CostEstimate(flops=flops, bytes_accessed=nbytes, transcendentals=0),
    )


def shape(dims, dtype):
    return jax.ShapeDtypeStruct(dims, dtype)


def dot_nt(a, b):
    return lax.dot_general(a, b, (((1,), (1,)), ((), ())), preferred_element_type=f32)


def position():
    r = lax.axis_index("row")
    return lax.axis_index("grp"), lax.shift_right_logical(r, 1), jnp.bitwise_and(r, 1)


def ahead_kernel(zero_ref):
    zero_ref[...] = jnp.zeros_like(zero_ref)


def ahead(dims):
    return call(ahead_kernel, [], [shape(dims, f32)], 1 << 20, 8 << 30, 24 << 20)()[0]


def mirror_kernel(rows_grp, cols_ref, tiles_ref, factor_ref, zero_ref, keep_ref, send_ref, stage):
    groups = tiles_ref.shape[0]
    half = rows_grp // 2
    slots = min(tiles_ref.shape[1], rows_grp)
    g, _, core = position()
    own = factor_ref[...]
    for h in range(groups):

        @pl.when(h <= g)
        def _():
            for u in range(2 * half):
                stage[u] = zero_ref[...]
            for s in range(slots):
                col = cols_ref[h, s]
                place = col - h * rows_grp
                side = jnp.bitwise_xor(jnp.bitwise_and(place, 1), core)
                unit = side * half + lax.shift_right_arithmetic(place, 1)
                unit = jnp.where(col >= 0, unit, 2 * half)
                stage[unit] = jnp.dot(own, tiles_ref[h, s], preferred_element_type=f32)
            keep_ref[h] = stage[0:half]
            send_ref[h] = stage[half : 2 * half]


def mirror(tiles, cols, factor, zero, rows_grp):
    groups, slots, tile, _ = tiles.shape
    rank = factor.shape[0]
    half = rows_grp // 2
    return call(
        functools.partial(mirror_kernel, rows_grp),
        [SMEM, VMEM, VMEM, VMEM],
        [shape((groups, half, rank, tile), f32)] * 2,
        12 << 20,
        2 * groups * slots * rank * tile * tile,
        groups * slots * tile * tile * 2,
        [pltpu.VMEM((2 * half + 1, rank, tile), f32)],
    )(cols, tiles, factor, zero)


LOWEST = -64
LADDER = (64, 32, 16, 8, 4, 2, 1)


def row_scale(top):
    power = jnp.full(top.shape, 2.0**LOWEST, f32)
    inverse = jnp.full(top.shape, 2.0**-LOWEST, f32)
    steps = jnp.zeros(top.shape, jnp.int32)
    for b in LADDER:
        up = top >= power * 2.0**b
        power = jnp.where(up, power * 2.0**b, power)
        inverse = jnp.where(up, inverse * 2.0**-b, inverse)
        steps = jnp.where(up, steps + b, steps)
    return inverse, steps


def row_power(steps):
    power = jnp.full(steps.shape, 2.0**LOWEST, f32)
    for b in LADDER:
        power = jnp.where(jnp.bitwise_and(steps, b) != 0, power * 2.0**b, power)
    return power


def encode(pay, values):
    rank = values[0].shape[0]
    mid = rank // 2
    top = functools.reduce(jnp.maximum, values)
    inverse, steps = row_scale(jnp.max(top, axis=1, keepdims=True))
    factor = inverse * 2.0**15
    for u, value in enumerate(values):
        q = jnp.minimum((value * factor + 0.5).astype(jnp.int32), 65535)
        pay[u * mid : (u + 1) * mid] = jnp.bitwise_or(q[:mid], lax.shift_left(q[mid:], 16))
    return steps


def decode(pay, u, power):
    mid = power.shape[0] // 2
    word = pay[u * mid : (u + 1) * mid]
    low = jnp.bitwise_and(word, 65535).astype(f32)
    high = jnp.bitwise_and(lax.shift_right_logical(word, 16), 65535).astype(f32)
    return jnp.concatenate([low, high], axis=0) * power


def put_steps(pay, *several):
    rank = several[0].shape[0]
    base, wide = pay.shape[0] - 8, pay.shape[1] * 8 // rank
    lanes = wide // len(several)
    for j, steps in enumerate(several):
        for i in range(rank // 8):
            at = i * wide + j * lanes
            pay[base:, at : at + lanes] = jnp.broadcast_to(steps[i * 8 : i * 8 + 8], (8, lanes))


def get_steps(pay, rank, j, of):
    base, wide = pay.shape[0] - 8, pay.shape[1] * 8 // rank
    at = [i * wide + j * (wide // of) for i in range(rank // 8)]
    return jnp.concatenate([pay[base:, k : k + 1] for k in at], axis=0)


def put_square(pay, base, square):
    rank = square.shape[0]
    rows = rank * rank // pay.shape[1]
    for j in range(rank // rows):
        pay[base : base + rows, j * rank : (j + 1) * rank] = square[j * rows : (j + 1) * rows]


def get_square(pay, base, rank):
    rows = rank * rank // pay.shape[1]
    return jnp.concatenate([pay[base : base + rows, j * rank : (j + 1) * rank] for j in range(rank // rows)], axis=0)


def pack_kernel(groups, half, keep_ref, recv_ref, *refs):
    rows, outs = refs[:half], refs[half:]
    own_ref, mine_ref, gram_ref = outs[:3]
    g, _, _ = position()
    rank = keep_ref.shape[2]
    gram = jnp.zeros((rank, rank), f32)
    for e in range(half):
        mine_ref[e] = rows[e][...]
        gram += dot_nt(rows[e][...], rows[e][...])
    gram_ref[...] = gram
    inverse, steps = row_scale(jnp.max(gram, axis=1, keepdims=True))
    coded = (gram * (inverse * 2.0**29) + 0.5).astype(jnp.int32)
    own_ref[...] = keep_ref[g] + recv_ref[g]
    for d in range(1, groups):
        pay = outs[2 + d]
        t = jnp.bitwise_xor(g, d)
        put_square(pay, half * rank // 2, coded)
        down = t < g
        sums = [keep_ref[t, u] + recv_ref[t, u] for u in range(half)]
        above = encode(pay, [jnp.where(down, sums[u], rows[u][...].astype(f32)) for u in range(half)])
        put_steps(pay, above, steps)


def pack(keep, recv, rows):
    groups, half, rank, tile = keep.shape
    return call(
        functools.partial(pack_kernel, groups, half),
        [VMEM, VMEM] + [VMEM] * half,
        [shape((half, rank, tile), f32), shape((half, rank, tile), bf16), shape((rank, rank), f32)]
        + [shape((half * rank // 2 + rank * rank // tile + 8, tile), jnp.int32)] * (groups - 1),
        16 << 20,
        keep.size * 4,
        keep.size * 8,
    )(keep, recv, *rows)


def split3(value):
    hi = value.astype(bf16)
    rest = value - hi.astype(f32)
    mid = rest.astype(bf16)
    low = (rest - mid.astype(f32)).astype(bf16)
    return hi, mid, low


def merge_kernel(groups, half, own_ref, gram_ref, *refs):
    g, z, _ = position()
    arrived = refs[: groups - 1]
    outs = refs[groups - 1 : groups - 1 + half]
    heard_ref, total_ref, acc = refs[groups - 1 + half :]
    rank = own_ref.shape[1]
    gram = gram_ref[...]
    sums = [own_ref[u] for u in range(half)]
    for d in range(1, groups):
        pay = arrived[d - 1]
        power = row_power(get_steps(pay, rank, 1, 2)) * 2.0**-29
        gram += get_square(pay, half * rank // 2, rank).astype(f32) * power
        power = row_power(get_steps(pay, rank, 0, 2)) * 2.0**-15
        above = jnp.bitwise_xor(g, d) > g
        for u in range(half):
            value = decode(pay, u, power)
            sums[u] += jnp.where(above, value, 0.0)
            heard_ref[(d - 1) * half + u] = value.astype(bf16)

    total_ref[...] = gram
    for i, part in enumerate(split3(gram)):
        heard_ref[(groups - 1) * half, :, i * rank : (i + 1) * rank] = part
    for u in range(half):
        acc[u] = sums[u]
    outs[0][...] = acc[z]
    for e in range(1, half):
        put_steps(outs[e], encode(outs[e], [acc[jnp.bitwise_xor(z, e)]]))


def merge(own, gram, arrived):
    half, rank, tile = own.shape
    groups = len(arrived) + 1
    return call(
        functools.partial(merge_kernel, groups, half),
        [VMEM, VMEM] + [VMEM] * (groups - 1),
        [shape((rank, tile), f32)]
        + [shape((rank // 2 + 8, tile), jnp.int32)] * (half - 1)
        + [shape(((groups - 1) * half + 1, rank, tile), bf16), shape((rank, rank), f32)],
        16 << 20,
        own.size * 2 * groups,
        own.size * 4 * groups,
        [pltpu.VMEM((half, rank, tile), f32)],
    )(own, gram, *arrived)


def row_products(cols_ref, tiles_ref, held, h, base, rows_grp):
    _, z, core = position()
    half = rows_grp // 2
    total = None
    for s in range(min(tiles_ref.shape[1], rows_grp)):
        col = cols_ref[h, s]
        place = col - h * rows_grp
        side = jnp.bitwise_xor(jnp.bitwise_and(place, 1), core)
        unit = side * half + jnp.bitwise_xor(lax.shift_right_arithmetic(place, 1), z)
        x = held[jnp.where(col >= 0, base + unit, held.shape[0] - 1)]
        term = dot_nt(tiles_ref[h, s], x)
        total = term if total is None else total + term
    return total


def near_kernel(rows_grp, cols_ref, tiles_ref, mine_ref, theirs_ref, out_ref, held):
    g, _, _ = position()
    half = rows_grp // 2
    held[0:half] = mine_ref[...]
    held[half:rows_grp] = theirs_ref[...]
    held[rows_grp] = jnp.zeros_like(held[0])
    out_ref[...] = row_products(cols_ref, tiles_ref, held, g, 0, rows_grp)


def near(tiles, cols, mine, theirs, rows_grp):
    _, slots, tile, _ = tiles.shape
    rank = mine.shape[1]
    return call(
        functools.partial(near_kernel, rows_grp),
        [SMEM, VMEM, VMEM, VMEM],
        [shape((tile, rank), f32)],
        8 << 20,
        2 * slots * rank * tile * tile,
        slots * tile * tile * 2,
        [pltpu.VMEM((rows_grp + 1, rank, tile), bf16)],
    )(cols, tiles, mine, theirs)[0]


def lower_kernel(groups, rows_grp, cols_ref, tiles_ref, factor_ref, near_ref, part_ref, *refs):
    heard_ref, told_ref, out_ref, gram_ref, held, acc = refs
    half = rows_grp // 2
    rank = factor_ref.shape[0]
    g, _, _ = position()
    held[groups * rows_grp] = jnp.zeros_like(held[0])
    for d in range(1, groups):
        t = jnp.bitwise_xor(g, d)
        held[pl.ds(t * rows_grp, half)] = heard_ref[(d - 1) * half : d * half]
        held[pl.ds(t * rows_grp + half, half)] = told_ref[(d - 1) * half : d * half]

    gram = part_ref[...]
    for i in range(3):
        gram += told_ref[(groups - 1) * half, :, i * rank : (i + 1) * rank].astype(f32)
    gram_ref[...] = gram
    acc[...] = near_ref[...]
    for h in range(groups - 1):

        @pl.when(h < g)
        def _():
            acc[...] += row_products(cols_ref, tiles_ref, held, h, h * rows_grp, rows_grp)

    fitted = lax.dot_general(
        gram,
        factor_ref[...].astype(f32),
        (((0,), (0,)), ((), ())),
        precision=lax.Precision.HIGHEST,
        preferred_element_type=f32,
    )
    out_ref[...] = acc[...].T - fitted


def lower(tiles, cols, factor, first, part, heard, told, rows_grp):
    groups, slots, tile, _ = tiles.shape
    rank = factor.shape[0]
    return call(
        functools.partial(lower_kernel, groups, rows_grp),
        [SMEM] + [VMEM] * 6,
        [shape((rank, tile), f32), shape((rank, rank), f32)],
        20 << 20,
        2 * groups * slots * rank * tile * tile,
        groups * slots * tile * tile * 2,
        [pltpu.VMEM((groups * rows_grp + 1, rank, tile), bf16), pltpu.VMEM((tile, rank), f32)],
    )(cols, tiles, factor, first, part, heard, told)


def sweep_kernel(parts, base_ref, gram_ref, factor_ref, own_ref, *refs):
    out_ref = refs[parts]
    rank, tile = factor_ref.shape
    current = factor_ref[...].astype(f32)
    gram = gram_ref[...]
    residual = base_ref[...] + own_ref[...]
    for ref in refs[:parts]:
        residual += decode(ref, 0, row_power(get_steps(ref, rank, 0, 1)) * 2.0**-15)
    eye = lax.broadcasted_iota(jnp.int32, (rank, rank), 0) == lax.broadcasted_iota(jnp.int32, (rank, rank), 1)
    diagonal = jnp.sum(jnp.where(eye, gram, 0.0), axis=1, keepdims=True)
    inverse = 1.0 / diagonal
    step = 8
    blocks = rank // step
    place = lax.broadcasted_iota(jnp.int32, (step, tile), 0)
    rest = [residual[b * step : (b + 1) * step] for b in range(blocks)]
    for b in range(blocks):
        here = current[b * step : (b + 1) * step]
        inv = jnp.broadcast_to(inverse[b * step : (b + 1) * step], (step, tile))
        result = here
        for k in range(step):
            fresh = jnp.maximum(here + rest[b] * inv, floor_value)
            delta = jnp.broadcast_to((fresh - here)[k : k + 1], (step, tile))
            result = jnp.where(place == k, fresh, result)
            row = b * step + k
            for j in range(b, blocks):
                rest[j] = rest[j] - gram[j * step : (j + 1) * step, row : row + 1] * delta
        out_ref[b * step : (b + 1) * step] = result


def sweep(base, gram, factor, own, parts):
    rank, tile = factor.shape
    return call(
        functools.partial(sweep_kernel, len(parts)),
        [VMEM] * (4 + len(parts)),
        [shape((rank, tile), f32)],
        8 << 20,
        2 * rank * rank * tile,
        rank * tile * 4 * (len(parts) + 3),
    )(base, gram, factor, own, *parts)[0]


def per_device(blocks, columns, factor):
    tiles = blocks[0]
    cols = pltpu.with_memory_space_constraint(columns[0], pltpu.HBM)
    rows_grp = lax.axis_size("row")
    groups = lax.axis_size("grp")
    half = rows_grp // 2

    def over_z(x, e):
        return lax.ppermute(x, "row", [(i, ((i // 2) ^ e) * 2 + i % 2) for i in range(rows_grp)])

    def over_core(x):
        return lax.ppermute(x, "row", [(i, i ^ 1) for i in range(rows_grp)])

    def over_grp(x, d):
        return lax.ppermute(x, "grp", [(i, i ^ d) for i in range(groups)])

    zero = ahead(factor.shape)
    rows = [factor]
    for e in range(1, half):
        low = e & -e
        rows.append(over_z(rows[e - low], low))
    keep, send = mirror(tiles, cols, factor, zero, rows_grp)
    recv = over_core(send)
    own, mine, gram, *pays = pack(keep, recv, rows)
    arrived = [over_grp(pay, d + 1) for d, pay in enumerate(pays)]
    theirs = over_core(mine)
    first = near(tiles, cols, mine, theirs, rows_grp)
    *sums, heard, part = merge(own, gram, arrived)
    told = over_core(heard)
    parts = [over_z(sums[e], e) for e in range(1, half)]
    base, gram = lower(tiles, cols, factor, first, part, heard, told, rows_grp)
    return sweep(base, gram, factor, sums[0], parts)


def solution(mesh):
    in_specs = (
        P(("grp", "row"), None, None, None, None),
        P(("grp", "row"), None, None),
        P(None, ("grp", "row")),
    )
    out_specs = P(None, ("grp", "row"))
    return jax.shard_map(
        per_device, mesh=mesh, in_specs=in_specs, out_specs=out_specs, check_vma=False
    )
```

profile of v0, /device:TPU:0, one launch (start us, length us, event | category | flops | bytes accessed | tf_op | source)
XLA Modules:
  0.0 38.0 jit_solution(11717326908921745171)
XLA Ops:
  0.0 0.0 copy-start
  0.0 0.0 copy-start.1
  0.0 2.5 %copy-done = bf16[1,4,10,256,256]{4,3,2,1,0:T(8,128)(2,1)S(1)} copy-done((bf16[1,4,10,256,256]{4,3,2,1,0:T(8,128)(2,1)S(1)}, bf16[1,4,10,256,256]{4,3,2,1,0:T(8,128)(2,1)}, u32[]{:S(2)}) %copy-start) | copy-done | bytes 5242904
  2.5 0.0 copy-done.1
  2.5 1.0 %shard_map.38 = (f32[4,4,64,256]{3,2,1,0:T(8,128)S(1)}, f32[4,4,64,256]{3,2,1,0:T(8,128)S(1)}) custom-call(s32[4,10]{1,0:T(4,128)} %bitcast.5, bf16[4,10,256,256]{3,2,1,0:T(8,128)(2,1)S(1)} %bitcast.2, bf16[64,256]{1,0:T(8,128)(2,1)S(1)} %copy-done.1, f32[64,256]{1,0:T(8,128)S(1)} %shard_map.37.zero_ref), custom_call_target="tpu_custom_call" | custom-call | flops 335544320 | bytes 5242880 | tf_op jit(solution)/shard_map/pallas_call | solution.py:79
  3.5 0.6 %collective-permute-start = (f32[4,4,64,256]{3,2,1,0:T(8,128)S(1)}, f32[4,4,64,256]{3,2,1,0:T(8,128)S(1)}, u32[]{:S(2)}, u32[]{:S(2)}) collective-permute-start(f32[4,4,64,256]{3,2,1,0:T(8,128)S(1)} %get-tuple-element.22), channel_id=1, source_target_pairs={{0,1},{1,0},{2,3},{3,2},{4,5},{5,4},{6,7},{7,6},{8,9},{9,8},{10,11... | collective-permute-start | bytes 3145736 | tf_op jit(solution)/shard_map/ppermute | solution.py:386
  4.1 3.7 %collective-permute-start.2 = (bf16[64,256]{1,0:T(8,128)(2,1)S(1)}, bf16[64,256]{1,0:T(8,128)(2,1)S(1)}, u32[]{:S(2)}, u32[]{:S(2)}) collective-permute-start(bf16[64,256]{1,0:T(8,128)(2,1)S(1)} %copy-done.1), channel_id=1, source_target_pairs={{0,4},{1,5},{2,6},{3,7},{4,0},{5,1},{6,2},{7,3},{8,12},{9,13},{10,... | collective-permute-start | bytes 98312 | tf_op jit(solution)/shard_map/ppermute | solution.py:383
  7.8 1.6 %collective-permute-start.1 = (bf16[64,256]{1,0:T(8,128)(2,1)S(1)}, bf16[64,256]{1,0:T(8,128)(2,1)S(1)}, u32[]{:S(2)}, u32[]{:S(2)}) collective-permute-start(bf16[64,256]{1,0:T(8,128)(2,1)S(1)} %copy-done.1), channel_id=1, source_target_pairs={{0,2},{1,3},{2,0},{3,1},{4,6},{5,7},{6,4},{7,5},{8,10},{9,11},{10,... | collective-permute-start | bytes 98312 | tf_op jit(solution)/shard_map/ppermute | solution.py:383
  9.3 0.4 %collective-permute-done.2.refs_2_ = bf16[64,256]{1,0:T(8,128)(2,1)S(1)} collective-permute-done((bf16[64,256]{1,0:T(8,128)(2,1)S(1)}, bf16[64,256]{1,0:T(8,128)(2,1)S(1)}, u32[]{:S(2)}, u32[]{:S(2)}) %collective-permute-start.2) | collective-permute-done | bytes 32800 | tf_op jit(solution)/shard_map/ppermute | solution.py:383
  9.7 2.0 %collective-permute-start.3 = (bf16[64,256]{1,0:T(8,128)(2,1)S(1)}, bf16[64,256]{1,0:T(8,128)(2,1)S(1)}, u32[]{:S(2)}, u32[]{:S(2)}) collective-permute-start(bf16[64,256]{1,0:T(8,128)(2,1)S(1)} %collective-permute-done.2.refs_2_), channel_id=1, source_target_pairs={{0,2},{1,3},{2,0},{3,1},{4,6},{5,7},{6,4},{7,5},{8,10},{9,11},{10,... | collective-permute-start | bytes 98312 | tf_op jit(solution)/shard_map/ppermute | solution.py:383
  11.7 0.0 collective-permute-done.1.refs_1_
  11.7 1.9 %collective-permute-done.3.refs_3_ = bf16[64,256]{1,0:T(8,128)(2,1)S(1)} collective-permute-done((bf16[64,256]{1,0:T(8,128)(2,1)S(1)}, bf16[64,256]{1,0:T(8,128)(2,1)S(1)}, u32[]{:S(2)}, u32[]{:S(2)}) %collective-permute-start.3) | collective-permute-done | bytes 32800 | tf_op jit(solution)/shard_map/ppermute | solution.py:383
  13.7 0.0 collective-permute-done.recv_ref
  13.7 0.6 %shard_map.39 = (f32[4,64,256]{2,1,0:T(8,128)S(1)}, bf16[4,64,256]{2,1,0:T(8,128)(2,1)S(1)}, f32[64,64]{1,0:T(8,128)S(1)}, s32[152,256]{1,0:T(8,128)S(1)}, s32[1...) custom-call(f32[4,4,64,256]{3,2,1,0:T(8,128)S(1)} %get-tuple-element.21.keep_ref, ...), custom_call_target="tpu_custom_call" | custom-call | flops 1048576 | bytes 2097152 | tf_op jit(solution)/shard_map/pallas_call | solution.py:186
  14.3 2.1 %collective-permute-start.5 = (s32[152,256]{1,0:T(8,128)S(1)}, s32[152,256]{1,0:T(8,128)S(1)}, u32[]{:S(2)}, u32[]{:S(2)}) collective-permute-start(s32[152,256]{1,0:T(8,128)S(1)} %get-tuple-element.26), channel_id=1, source_target_pairs={{0,8},{8,0},{16,24},{24,16},{1,9},{9,1},{17,25},{25,17},{2,10},{10... | collective-permute-start | bytes 466952 | tf_op jit(solution)/shard_map/ppermute | solution.py:389
  16.4 2.2 %collective-permute-start.6 = (s32[152,256]{1,0:T(8,128)S(1)}, s32[152,256]{1,0:T(8,128)S(1)}, u32[]{:S(2)}, u32[]{:S(2)}) collective-permute-start(s32[152,256]{1,0:T(8,128)S(1)} %get-tuple-element.27), channel_id=1, source_target_pairs={{0,16},{8,24},{16,0},{24,8},{1,17},{9,25},{17,1},{25,9},{2,18},{10... | collective-permute-start | bytes 466952 | tf_op jit(solution)/shard_map/ppermute | solution.py:389
  18.6 0.0 collective-permute-start.7
  18.6 2.2 %collective-permute-done.5.refs_0_ = s32[152,256]{1,0:T(8,128)S(1)} collective-permute-done((s32[152,256]{1,0:T(8,128)S(1)}, s32[152,256]{1,0:T(8,128)S(1)}, u32[]{:S(2)}, u32[]{:S(2)}) %collective-permute-start.5) | collective-permute-done | bytes 155680 | tf_op jit(solution)/shard_map/ppermute | solution.py:389
  20.8 4.1 %collective-permute-done.6.refs_1_ = s32[152,256]{1,0:T(8,128)S(1)} collective-permute-done((s32[152,256]{1,0:T(8,128)S(1)}, s32[152,256]{1,0:T(8,128)S(1)}, u32[]{:S(2)}, u32[]{:S(2)}) %collective-permute-start.6) | collective-permute-done | bytes 155680 | tf_op jit(solution)/shard_map/ppermute | solution.py:389
  24.9 0.0 collective-permute-done.7.refs_2_
  24.9 0.6 %shard_map.41 = (f32[64,256]{1,0:T(8,128)S(1)}, s32[40,256]{1,0:T(8,128)S(1)}, s32[40,256]{1,0:T(8,128)S(1)}, s32[40,256]{1,0:T(8,128)S(1)}, bf16[13,64,256]{2,1,0:T(8,128)(2,1)S(1)}, /*index=5*/f32[64,64]{1,0:T(8,128)S(1)}) custom-call(f32[4,64,256]{2,1,0:T(8,128)S(1)} %get-tuple-element.24.own_ref, f32[64,64]{1,0:T(8,128)S(1)} %get-tuple-element.25.gram_ref, ...), custom_call_target="tpu_custom_call" | custom-call | flops 524288 | bytes 1048576 | tf_op jit(solution)/shard_map/pallas_call | solution.py:237
  25.5 0.1 collective-permute-start.8
  25.5 0.5 %collective-permute-start.4 = (bf16[4,64,256]{2,1,0:T(8,128)(2,1)S(1)}, bf16[4,64,256]{2,1,0:T(8,128)(2,1)S(1)}, u32[]{:S(2)}, u32[]{:S(2)}) collective-permute-start(bf16[4,64,256]{2,1,0:T(8,128)(2,1)S(1)} %get-tuple-element.23.mine_ref), channel_id=1, source_target_pairs={{0,1},{1,0},{2,3},{3,2},{4,5},{5,4},{6,7},{7,6},{8,9},{9,8},{10,11... | collective-permute-start | bytes 393224 | tf_op jit(solution)/shard_map/ppermute | solution.py:386
  26.0 1.6 %collective-permute-start.9 = (s32[40,256]{1,0:T(8,128)S(1)}, s32[40,256]{1,0:T(8,128)S(1)}, u32[]{:S(2)}, u32[]{:S(2)}) collective-permute-start(s32[40,256]{1,0:T(8,128)S(1)} %get-tuple-element.34), channel_id=1, source_target_pairs={{0,2},{1,3},{2,0},{3,1},{4,6},{5,7},{6,4},{7,5},{8,10},{9,11},{10,... | collective-permute-start | bytes 122888 | tf_op jit(solution)/shard_map/ppermute | solution.py:383
  27.6 3.2 %collective-permute-start.10 = (s32[40,256]{1,0:T(8,128)S(1)}, s32[40,256]{1,0:T(8,128)S(1)}, u32[]{:S(2)}, u32[]{:S(2)}) collective-permute-start(s32[40,256]{1,0:T(8,128)S(1)} %get-tuple-element.35), channel_id=1, source_target_pairs={{0,4},{1,5},{2,6},{3,7},{4,0},{5,1},{6,2},{7,3},{8,12},{9,13},{10,... | collective-permute-start | bytes 122888 | tf_op jit(solution)/shard_map/ppermute | solution.py:383
  30.9 0.0 collective-permute-start.11
  30.9 0.0 collective-permute-done.4.theirs_ref
  30.9 1.1 %shard_map.40.near_ref = f32[256,64]{1,0:T(8,128)S(1)} custom-call(s32[4,10]{1,0:T(4,128)} %bitcast.6, bf16[4,10,256,256]{3,2,1,0:T(8,128)(2,1)S(1)} %bitcast.3, bf16[4,64,256]{2,1,0:T(8,128)(2,1)S(1)} %get-tuple-element.23.mine_ref, bf16[4,64,256]{2,1,0:T(8,128)(2,1)S(1)} %collective-permute-done.4.theirs_ref), custom_call_target="tpu_custom_call" | custom-call | flops 83886080 | bytes 1310720 | tf_op jit(solution)/shard_map/pallas_call | solution.py:277
  32.0 0.0 collective-permute-done.8.refs_1_
  32.0 1.0 %shard_map.42 = (f32[64,256]{1,0:T(8,128)S(1)}, f32[64,64]{1,0:T(8,128)S(1)}) custom-call(s32[4,10]{1,0:T(4,128)} %bitcast.7, bf16[4,10,256,256]{3,2,1,0:T(8,128)(2,1)S(1)} %bitcast.4, bf16[64,256]{1,0:T(8,128)(2,1)S(1)} %copy-done.1, f32[256,64]{1,0:T(8,128)S(1)} %shard_map.40.near_ref, f32[64,64]{1,0:T(8,128)S(1)} %get-tuple-element.29.part_ref, ...), custom_call_target="tpu_custom_call" | custom-call | flops 335544320 | bytes 5242880 | tf_op jit(solution)/shard_map/pallas_call | solution.py:323
  33.1 0.0 collective-permute-done.9.refs_0_
  33.1 0.5 %collective-permute-done.10.refs_1_ = s32[40,256]{1,0:T(8,128)S(1)} collective-permute-done((s32[40,256]{1,0:T(8,128)S(1)}, s32[40,256]{1,0:T(8,128)S(1)}, u32[]{:S(2)}, u32[]{:S(2)}) %collective-permute-start.10) | collective-permute-done | bytes 40992 | tf_op jit(solution)/shard_map/ppermute | solution.py:383
  33.6 3.1 %collective-permute-done.11.refs_2_ = s32[40,256]{1,0:T(8,128)S(1)} collective-permute-done((s32[40,256]{1,0:T(8,128)S(1)}, s32[40,256]{1,0:T(8,128)S(1)}, u32[]{:S(2)}, u32[]{:S(2)}) %collective-permute-start.11) | collective-permute-done | bytes 40992 | tf_op jit(solution)/shard_map/ppermute | solution.py:383
  36.7 1.3 %shard_map.43 = f32[64,256]{1,0:T(8,128)} custom-call(f32[64,256]{1,0:T(8,128)S(1)} %get-tuple-element.31.base_ref, f32[64,64]{1,0:T(8,128)S(1)} %get-tuple-element.32.gram_ref, bf16[64,256]{1,0:T(8,128)(2,1)S(1)} %copy-done.1, f32[64,256]{1,0:T(8,128)S(1)} %get-tuple-element.33.own_ref, s32[40,256]{1,0:T(8,128)S(1)} %collective-permute-done.9.refs_0_, ...), custom_call_target="tpu_custom_call" | custom-call | flops 2097152 | bytes 393216 | tf_op jit(solution)/shard_map/pallas_call | solution.py:365
  (1 shorter events, 0.0 us)
Async XLA Ops:
  0.0 2.5 %copy-start = (bf16[1,4,10,256,256]{4,3,2,1,0:T(8,128)(2,1)S(1)}, bf16[1,4,10,256,256]{4,3,2,1,0:T(8,128)(2,1)}, u32[]{:S(2)}) copy-start(bf16[1,4,10,256,256]{4,3,2,1,0:T(8,128)(2,1)} %param.3) | copy-start | bytes 15728644
  0.0 2.5 %copy-start.1 = (bf16[64,256]{1,0:T(8,128)(2,1)S(1)}, bf16[64,256]{1,0:T(8,128)(2,1)}, u32[]{:S(2)}) copy-start(bf16[64,256]{1,0:T(8,128)(2,1)} %factor_ref.5) | copy-start | bytes 98308
  3.5 10.1 %collective-permute-start = (f32[4,4,64,256]{3,2,1,0:T(8,128)S(1)}, f32[4,4,64,256]{3,2,1,0:T(8,128)S(1)}, u32[]{:S(2)}, u32[]{:S(2)}) collective-permute-start(f32[4,4,64,256]{3,2,1,0:T(8,128)S(1)} %get-tuple-element.22), channel_id=1, source_target_pairs={{0,1},{1,0},{2,3},{3,2},{4,5},{5,4},{6,7},{7,6},{8,9},{9,8},{10,11... | collective-permute-start | bytes 3145736 | tf_op jit(solution)/shard_map/ppermute | solution.py:386
  4.1 5.6 %collective-permute-start.2 = (bf16[64,256]{1,0:T(8,128)(2,1)S(1)}, bf16[64,256]{1,0:T(8,128)(2,1)S(1)}, u32[]{:S(2)}, u32[]{:S(2)}) collective-permute-start(bf16[64,256]{1,0:T(8,128)(2,1)S(1)} %copy-done.1), channel_id=1, source_target_pairs={{0,4},{1,5},{2,6},{3,7},{4,0},{5,1},{6,2},{7,3},{8,12},{9,13},{10,... | collective-permute-start | bytes 98312 | tf_op jit(solution)/shard_map/ppermute | solution.py:383
  7.8 4.0 %collective-permute-start.1 = (bf16[64,256]{1,0:T(8,128)(2,1)S(1)}, bf16[64,256]{1,0:T(8,128)(2,1)S(1)}, u32[]{:S(2)}, u32[]{:S(2)}) collective-permute-start(bf16[64,256]{1,0:T(8,128)(2,1)S(1)} %copy-done.1), channel_id=1, source_target_pairs={{0,2},{1,3},{2,0},{3,1},{4,6},{5,7},{6,4},{7,5},{8,10},{9,11},{10,... | collective-permute-start | bytes 98312 | tf_op jit(solution)/shard_map/ppermute | solution.py:383
  9.7 3.9 %collective-permute-start.3 = (bf16[64,256]{1,0:T(8,128)(2,1)S(1)}, bf16[64,256]{1,0:T(8,128)(2,1)S(1)}, u32[]{:S(2)}, u32[]{:S(2)}) collective-permute-start(bf16[64,256]{1,0:T(8,128)(2,1)S(1)} %collective-permute-done.2.refs_2_), channel_id=1, source_target_pairs={{0,2},{1,3},{2,0},{3,1},{4,6},{5,7},{6,4},{7,5},{8,10},{9,11},{10,... | collective-permute-start | bytes 98312 | tf_op jit(solution)/shard_map/ppermute | solution.py:383
  14.3 6.5 %collective-permute-start.5 = (s32[152,256]{1,0:T(8,128)S(1)}, s32[152,256]{1,0:T(8,128)S(1)}, u32[]{:S(2)}, u32[]{:S(2)}) collective-permute-start(s32[152,256]{1,0:T(8,128)S(1)} %get-tuple-element.26), channel_id=1, source_target_pairs={{0,8},{8,0},{16,24},{24,16},{1,9},{9,1},{17,25},{25,17},{2,10},{10... | collective-permute-start | bytes 466952 | tf_op jit(solution)/shard_map/ppermute | solution.py:389
  16.4 8.4 %collective-permute-start.6 = (s32[152,256]{1,0:T(8,128)S(1)}, s32[152,256]{1,0:T(8,128)S(1)}, u32[]{:S(2)}, u32[]{:S(2)}) collective-permute-start(s32[152,256]{1,0:T(8,128)S(1)} %get-tuple-element.27), channel_id=1, source_target_pairs={{0,16},{8,24},{16,0},{24,8},{1,17},{9,25},{17,1},{25,9},{2,18},{10... | collective-permute-start | bytes 466952 | tf_op jit(solution)/shard_map/ppermute | solution.py:389
  18.6 6.3 %collective-permute-start.7 = (s32[152,256]{1,0:T(8,128)S(1)}, s32[152,256]{1,0:T(8,128)S(1)}, u32[]{:S(2)}, u32[]{:S(2)}) collective-permute-start(s32[152,256]{1,0:T(8,128)S(1)} %get-tuple-element.28), channel_id=1, source_target_pairs={{0,24},{8,16},{16,8},{24,0},{1,25},{9,17},{17,9},{25,1},{2,26},{10... | collective-permute-start | bytes 466952 | tf_op jit(solution)/shard_map/ppermute | solution.py:389
  25.5 6.6 %collective-permute-start.8 = (bf16[13,64,256]{2,1,0:T(8,128)(2,1)S(1)}, bf16[13,64,256]{2,1,0:T(8,128)(2,1)S(1)}, u32[]{:S(2)}, u32[]{:S(2)}) collective-permute-start(bf16[13,64,256]{2,1,0:T(8,128)(2,1)S(1)} %get-tuple-element.30.refs_0_), channel_id=1, source_target_pairs={{0,1},{1,0},{2,3},{3,2},{4,5},{5,4},{6,7},{7,6},{8,9},{9,8},{10,11... | collective-permute-start | bytes 1277960 | tf_op jit(solution)/shard_map/ppermute | solution.py:386
  25.5 5.4 %collective-permute-start.4 = (bf16[4,64,256]{2,1,0:T(8,128)(2,1)S(1)}, bf16[4,64,256]{2,1,0:T(8,128)(2,1)S(1)}, u32[]{:S(2)}, u32[]{:S(2)}) collective-permute-start(bf16[4,64,256]{2,1,0:T(8,128)(2,1)S(1)} %get-tuple-element.23.mine_ref), channel_id=1, source_target_pairs={{0,1},{1,0},{2,3},{3,2},{4,5},{5,4},{6,7},{7,6},{8,9},{9,8},{10,11... | collective-permute-start | bytes 393224 | tf_op jit(solution)/shard_map/ppermute | solution.py:386
  26.0 7.0 %collective-permute-start.9 = (s32[40,256]{1,0:T(8,128)S(1)}, s32[40,256]{1,0:T(8,128)S(1)}, u32[]{:S(2)}, u32[]{:S(2)}) collective-permute-start(s32[40,256]{1,0:T(8,128)S(1)} %get-tuple-element.34), channel_id=1, source_target_pairs={{0,2},{1,3},{2,0},{3,1},{4,6},{5,7},{6,4},{7,5},{8,10},{9,11},{10,... | collective-permute-start | bytes 122888 | tf_op jit(solution)/shard_map/ppermute | solution.py:383
  27.6 6.0 %collective-permute-start.10 = (s32[40,256]{1,0:T(8,128)S(1)}, s32[40,256]{1,0:T(8,128)S(1)}, u32[]{:S(2)}, u32[]{:S(2)}) collective-permute-start(s32[40,256]{1,0:T(8,128)S(1)} %get-tuple-element.35), channel_id=1, source_target_pairs={{0,4},{1,5},{2,6},{3,7},{4,0},{5,1},{6,2},{7,3},{8,12},{9,13},{10,... | collective-permute-start | bytes 122888 | tf_op jit(solution)/shard_map/ppermute | solution.py:383
  30.9 5.8 %collective-permute-start.11 = (s32[40,256]{1,0:T(8,128)S(1)}, s32[40,256]{1,0:T(8,128)S(1)}, u32[]{:S(2)}, u32[]{:S(2)}) collective-permute-start(s32[40,256]{1,0:T(8,128)S(1)} %get-tuple-element.36), channel_id=1, source_target_pairs={{0,6},{1,7},{2,4},{3,5},{4,2},{5,3},{6,0},{7,1},{8,14},{9,15},{10,... | collective-permute-start | bytes 122888 | tf_op jit(solution)/shard_map/ppermute | solution.py:383
where the time goes:
time: 38.2 us; the launch traced here: 38 us
  starting transfers between devices  17.5 us (46%)
  waiting for transfers between devices  12.2 us (32%)
  Pallas kernels  5.72 us (15%)
  local copies, waits for them, and re-layouts  2.48 us (6%)
    ppermute x6, starting transfers between devices, over_z(): lax.ppermute(x, 'row', [(i, (i // 2 ^ e) * 2 + i % 2) for i in range(rows...  12.1 us
    ppermute x3, waiting for transfers between devices, over_grp(): return lax.ppermute(x, 'grp', [(i, i ^ d) for i in range(groups)])  6.25 us
    ppermute x6, waiting for transfers between devices, over_z(): lax.ppermute(x, 'row', [(i, (i // 2 ^ e) * 2 + i % 2) for i in range(rows...  5.95 us
    ppermute x3, starting transfers between devices, over_grp(): return lax.ppermute(x, 'grp', [(i, i ^ d) for i in range(groups)])  4.32 us
    unnamed x4, local copies, waits for them, and re-layouts  2.48 us
    pallas_call x1, Pallas kernels, sweep(): call(functools.partial(sweep_kernel, len(parts)), [VMEM] * (4 + len(parts...  1.31 us
    ppermute x3, starting transfers between devices, over_core(): return lax.ppermute(x, 'row', [(i, i ^ 1) for i in range(rows_grp)])  1.13 us
    pallas_call x1, Pallas kernels, near(): call(functools.partial(near_kernel, rows_grp), [SMEM, VMEM, VMEM, VMEM],...  1.12 us
  transfers between devices with their start and end apart: 12, of which 6 were waited for; matrix products, arithmetic and copies ran while one was open for 0% of the time, Pallas kernels for 6%

commit v1 on v0

--- a/solution.py
+++ b/solution.py
@@ -118,32 +118,32 @@
     factor = inverse * 2.0**15
     for u, value in enumerate(values):
         q = jnp.minimum((value * factor + 0.5).astype(jnp.int32), 65535)
-        pay[u * mid : (u + 1) * mid] = jnp.bitwise_or(q[:mid], lax.shift_left(q[mid:], 16))
+        word = jnp.bitwise_or(q[:mid], lax.shift_left(q[mid:], 16))
+        width = pay.shape[1]
+        for j in range(word.shape[1] // width):
+            at = (u * word.shape[1] // width + j) * mid
+            pay[at : at + mid] = word[:, j * width : (j + 1) * width]
     return steps
 
 
-def decode(pay, u, power):
+def decode(pay, u, power, across=1):
     mid = power.shape[0] // 2
-    word = pay[u * mid : (u + 1) * mid]
+    word = jnp.concatenate([pay[(u + j) * mid : (u + j + 1) * mid] for j in range(across)], axis=1)
     low = jnp.bitwise_and(word, 65535).astype(f32)
     high = jnp.bitwise_and(lax.shift_right_logical(word, 16), 65535).astype(f32)
     return jnp.concatenate([low, high], axis=0) * power
 
 
-def put_steps(pay, *several):
-    rank = several[0].shape[0]
+def put_steps(pay, steps):
+    rank = steps.shape[0]
     base, wide = pay.shape[0] - 8, pay.shape[1] * 8 // rank
-    lanes = wide // len(several)
-    for j, steps in enumerate(several):
-        for i in range(rank // 8):
-            at = i * wide + j * lanes
-            pay[base:, at : at + lanes] = jnp.broadcast_to(steps[i * 8 : i * 8 + 8], (8, lanes))
-
-
-def get_steps(pay, rank, j, of):
+    for i in range(rank // 8):
+        pay[base:, i * wide : i * wide + wide] = jnp.broadcast_to(steps[i * 8 : i * 8 + 8], (8, wide))
+
+
+def get_steps(pay, rank):
     base, wide = pay.shape[0] - 8, pay.shape[1] * 8 // rank
-    at = [i * wide + j * (wide // of) for i in range(rank // 8)]
-    return jnp.concatenate([pay[base:, k : k + 1] for k in at], axis=0)
+    return jnp.concatenate([pay[base:, i * wide : i * wide + 1] for i in range(rank // 8)], axis=0)
 
 
 def put_square(pay, base, square):
@@ -169,16 +169,17 @@
         gram += dot_nt(rows[e][...], rows[e][...])
     gram_ref[...] = gram
     inverse, steps = row_scale(jnp.max(gram, axis=1, keepdims=True))
-    coded = (gram * (inverse * 2.0**29) + 0.5).astype(jnp.int32)
+    coded = jnp.minimum((gram * (inverse * 2.0**23) + 0.5).astype(jnp.int32), (1 << 24) - 1)
+    first = lax.broadcasted_iota(jnp.int32, (rank, rank), 1) == 0
     own_ref[...] = keep_ref[g] + recv_ref[g]
     for d in range(1, groups):
         pay = outs[2 + d]
         t = jnp.bitwise_xor(g, d)
-        put_square(pay, half * rank // 2, coded)
         down = t < g
         sums = [keep_ref[t, u] + recv_ref[t, u] for u in range(half)]
         above = encode(pay, [jnp.where(down, sums[u], rows[u][...].astype(f32)) for u in range(half)])
-        put_steps(pay, above, steps)
+        exponents = lax.shift_left(jnp.where(first, above, steps), 24)
+        put_square(pay, half * rank // 2, jnp.bitwise_or(coded, exponents))
 
 
 def pack(keep, recv, rows):
@@ -187,7 +188,7 @@
         functools.partial(pack_kernel, groups, half),
         [VMEM, VMEM] + [VMEM] * half,
         [shape((half, rank, tile), f32), shape((half, rank, tile), bf16), shape((rank, rank), f32)]
-        + [shape((half * rank // 2 + rank * rank // tile + 8, tile), jnp.int32)] * (groups - 1),
+        + [shape((half * rank // 2 + rank * rank // tile, tile), jnp.int32)] * (groups - 1),
         16 << 20,
         keep.size * 4,
         keep.size * 8,
@@ -212,9 +213,10 @@
     sums = [own_ref[u] for u in range(half)]
     for d in range(1, groups):
         pay = arrived[d - 1]
-        power = row_power(get_steps(pay, rank, 1, 2)) * 2.0**-29
-        gram += get_square(pay, half * rank // 2, rank).astype(f32) * power
-        power = row_power(get_steps(pay, rank, 0, 2)) * 2.0**-15
+        square = get_square(pay, half * rank // 2, rank)
+        exponents = lax.shift_right_logical(square, 24)
+        gram += jnp.bitwise_and(square, (1 << 24) - 1).astype(f32) * (row_power(exponents[:, 1:2]) * 2.0**-23)
+        power = row_power(exponents[:, 0:1]) * 2.0**-15
         above = jnp.bitwise_xor(g, d) > g
         for u in range(half):
             value = decode(pay, u, power)
@@ -238,7 +240,7 @@
         functools.partial(merge_kernel, groups, half),
         [VMEM, VMEM] + [VMEM] * (groups - 1),
         [shape((rank, tile), f32)]
-        + [shape((rank // 2 + 8, tile), jnp.int32)] * (half - 1)
+        + [shape((rank // 2 * (tile // 128) + 8, 128), jnp.int32)] * (half - 1)
         + [shape(((groups - 1) * half + 1, rank, tile), bf16), shape((rank, rank), f32)],
         16 << 20,
         own.size * 2 * groups,
@@ -286,7 +288,9 @@
 
 
 def lower_kernel(groups, rows_grp, cols_ref, tiles_ref, factor_ref, near_ref, part_ref, *refs):
-    heard_ref, told_ref, out_ref, gram_ref, held, acc = refs
+    heard_ref, told_ref, out_ref, gram_ref, held, acc, cols, sem = refs
+    fetch = pltpu.make_async_copy(cols_ref, cols, sem)
+    fetch.start()
     half = rows_grp // 2
     rank = factor_ref.shape[0]
     g, _, _ = position()
@@ -300,13 +304,6 @@
     for i in range(3):
         gram += told_ref[(groups - 1) * half, :, i * rank : (i + 1) * rank].astype(f32)
     gram_ref[...] = gram
-    acc[...] = near_ref[...]
-    for h in range(groups - 1):
-
-        @pl.when(h < g)
-        def _():
-            acc[...] += row_products(cols_ref, tiles_ref, held, h, h * rows_grp, rows_grp)
-
     fitted = lax.dot_general(
         gram,
         factor_ref[...].astype(f32),
@@ -314,6 +311,14 @@
         precision=lax.Precision.HIGHEST,
         preferred_element_type=f32,
     )
+    acc[...] = near_ref[...]
+    fetch.wait()
+    for h in range(groups - 1):
+
+        @pl.when(h < g)
+        def _():
+            acc[...] += row_products(cols, tiles_ref, held, h, h * rows_grp, rows_grp)
+
     out_ref[...] = acc[...].T - fitted
 
 
@@ -322,12 +327,17 @@
     rank = factor.shape[0]
     return call(
         functools.partial(lower_kernel, groups, rows_grp),
-        [SMEM] + [VMEM] * 6,
+        [HBM] + [VMEM] * 6,
         [shape((rank, tile), f32), shape((rank, rank), f32)],
         20 << 20,
         2 * groups * slots * rank * tile * tile,
         groups * slots * tile * tile * 2,
-        [pltpu.VMEM((groups * rows_grp + 1, rank, tile), bf16), pltpu.VMEM((tile, rank), f32)],
+        [
+            pltpu.VMEM((groups * rows_grp + 1, rank, tile), bf16),
+            pltpu.VMEM((tile, rank), f32),
+            pltpu.SMEM(cols.shape, jnp.int32),
+            pltpu.SemaphoreType.DMA(()),
+        ],
     )(cols, tiles, factor, first, part, heard, told)
 
 
@@ -338,26 +348,26 @@
     gram = gram_ref[...]
     residual = base_ref[...] + own_ref[...]
     for ref in refs[:parts]:
-        residual += decode(ref, 0, row_power(get_steps(ref, rank, 0, 1)) * 2.0**-15)
+        residual += decode(ref, 0, row_power(get_steps(ref, rank)) * 2.0**-15, tile // 128)
     eye = lax.broadcasted_iota(jnp.int32, (rank, rank), 0) == lax.broadcasted_iota(jnp.int32, (rank, rank), 1)
-    diagonal = jnp.sum(jnp.where(eye, gram, 0.0), axis=1, keepdims=True)
-    inverse = 1.0 / diagonal
+    inverse = 1.0 / jnp.sum(jnp.where(eye, gram, 0.0), axis=1, keepdims=True)
+    scaled = gram * inverse
+    residual = residual * inverse
+    least = floor_value - current
     step = 8
     blocks = rank // step
     place = lax.broadcasted_iota(jnp.int32, (step, tile), 0)
     rest = [residual[b * step : (b + 1) * step] for b in range(blocks)]
     for b in range(blocks):
-        here = current[b * step : (b + 1) * step]
-        inv = jnp.broadcast_to(inverse[b * step : (b + 1) * step], (step, tile))
-        result = here
+        at = slice(b * step, (b + 1) * step)
+        found = rest[b]
         for k in range(step):
-            fresh = jnp.maximum(here + rest[b] * inv, floor_value)
-            delta = jnp.broadcast_to((fresh - here)[k : k + 1], (step, tile))
-            result = jnp.where(place == k, fresh, result)
             row = b * step + k
+            found = jnp.where(place == k, rest[b], found)
+            delta = jnp.broadcast_to(jnp.maximum(rest[b], least[at])[k : k + 1], (step, tile))
             for j in range(b, blocks):
-                rest[j] = rest[j] - gram[j * step : (j + 1) * step, row : row + 1] * delta
-        out_ref[b * step : (b + 1) * step] = result
+                rest[j] = rest[j] - scaled[j * step : (j + 1) * step, row : row + 1] * delta
+        out_ref[at] = jnp.maximum(current[at] + found, floor_value)
 
 
 def sweep(base, gram, factor, own, parts):

time: 38.2 us -> 37.8 us (0.990)
  transfers between devices with their start and end apart: 12 -> 12, of which waited for: 6 -> 7; matrix products, arithmetic and copies ran while one was open for 0% -> 0% of each run, Pallas kernels for 6% -> 5%
where the time goes in v1:
time: 37.8 us; the launch traced here: 37.6 us
  starting transfers between devices  17.4 us (46%)
  waiting for transfers between devices  12.1 us (32%)
  Pallas kernels  5.62 us (15%)
  local copies, waits for them, and re-layouts  2.48 us (7%)
    ppermute x6, starting transfers between devices, over_z(): lax.ppermute(x, 'row', [(i, (i // 2 ^ e) * 2 + i % 2) for i in range(rows...  12 us
    ppermute x3, waiting for transfers between devices, over_grp(): return lax.ppermute(x, 'grp', [(i, i ^ d) for i in range(groups)])  6.04 us
    ppermute x6, waiting for transfers between devices, over_z(): lax.ppermute(x, 'row', [(i, (i // 2 ^ e) * 2 + i % 2) for i in range(rows...  6.01 us
    ppermute x3, starting transfers between devices, over_grp(): return lax.ppermute(x, 'grp', [(i, i ^ d) for i in range(groups)])  4.27 us
    unnamed x4, local copies, waits for them, and re-layouts  2.48 us
    pallas_call x1, Pallas kernels, sweep(): call(functools.partial(sweep_kernel, len(parts)), [VMEM] * (4 + len(parts...  1.27 us
    ppermute x3, starting transfers between devices, over_core(): return lax.ppermute(x, 'row', [(i, i ^ 1) for i in range(rows_grp)])  1.13 us
    pallas_call x1, Pallas kernels, near(): call(functools.partial(near_kernel, rows_grp), [SMEM, VMEM, VMEM, VMEM],...  1.12 us
  transfers between devices with their start and end apart: 12, of which 7 were waited for; matrix products, arithmetic and copies ran while one was open for 0% of the time, Pallas kernels for 5%

profile of v1, /device:TPU:0, one launch (start us, length us, event | category | flops | bytes accessed | tf_op | source)
XLA Modules:
  0.0 37.6 jit_solution(13942214432742895941)
XLA Ops:
  0.0 0.0 copy-start
  0.0 0.0 copy-start.1
  0.0 2.5 %copy-done = bf16[1,4,10,256,256]{4,3,2,1,0:T(8,128)(2,1)S(1)} copy-done((bf16[1,4,10,256,256]{4,3,2,1,0:T(8,128)(2,1)S(1)}, bf16[1,4,10,256,256]{4,3,2,1,0:T(8,128)(2,1)}, u32[]{:S(2)}) %copy-start) | copy-done | bytes 5242904
  2.5 0.0 copy-done.1
  2.5 1.0 %shard_map.38 = (f32[4,4,64,256]{3,2,1,0:T(8,128)S(1)}, f32[4,4,64,256]{3,2,1,0:T(8,128)S(1)}) custom-call(s32[4,10]{1,0:T(4,128)} %bitcast.5, bf16[4,10,256,256]{3,2,1,0:T(8,128)(2,1)S(1)} %bitcast.2, bf16[64,256]{1,0:T(8,128)(2,1)S(1)} %copy-done.1, f32[64,256]{1,0:T(8,128)S(1)} %shard_map.37.zero_ref), custom_call_target="tpu_custom_call" | custom-call | flops 335544320 | bytes 5242880 | tf_op jit(solution)/shard_map/pallas_call | solution.py:79
  3.5 0.6 %collective-permute-start = (f32[4,4,64,256]{3,2,1,0:T(8,128)S(1)}, f32[4,4,64,256]{3,2,1,0:T(8,128)S(1)}, u32[]{:S(2)}, u32[]{:S(2)}) collective-permute-start(f32[4,4,64,256]{3,2,1,0:T(8,128)S(1)} %get-tuple-element.22), channel_id=1, source_target_pairs={{0,1},{1,0},{2,3},{3,2},{4,5},{5,4},{6,7},{7,6},{8,9},{9,8},{10,11... | collective-permute-start | bytes 3145736 | tf_op jit(solution)/shard_map/ppermute | solution.py:396
  4.1 3.7 %collective-permute-start.2 = (bf16[64,256]{1,0:T(8,128)(2,1)S(1)}, bf16[64,256]{1,0:T(8,128)(2,1)S(1)}, u32[]{:S(2)}, u32[]{:S(2)}) collective-permute-start(bf16[64,256]{1,0:T(8,128)(2,1)S(1)} %copy-done.1), channel_id=1, source_target_pairs={{0,4},{1,5},{2,6},{3,7},{4,0},{5,1},{6,2},{7,3},{8,12},{9,13},{10,... | collective-permute-start | bytes 98312 | tf_op jit(solution)/shard_map/ppermute | solution.py:393
  7.8 1.6 %collective-permute-start.1 = (bf16[64,256]{1,0:T(8,128)(2,1)S(1)}, bf16[64,256]{1,0:T(8,128)(2,1)S(1)}, u32[]{:S(2)}, u32[]{:S(2)}) collective-permute-start(bf16[64,256]{1,0:T(8,128)(2,1)S(1)} %copy-done.1), channel_id=1, source_target_pairs={{0,2},{1,3},{2,0},{3,1},{4,6},{5,7},{6,4},{7,5},{8,10},{9,11},{10,... | collective-permute-start | bytes 98312 | tf_op jit(solution)/shard_map/ppermute | solution.py:393
  9.3 0.4 %collective-permute-done.2.refs_2_ = bf16[64,256]{1,0:T(8,128)(2,1)S(1)} collective-permute-done((bf16[64,256]{1,0:T(8,128)(2,1)S(1)}, bf16[64,256]{1,0:T(8,128)(2,1)S(1)}, u32[]{:S(2)}, u32[]{:S(2)}) %collective-permute-start.2) | collective-permute-done | bytes 32800 | tf_op jit(solution)/shard_map/ppermute | solution.py:393
  9.7 2.0 %collective-permute-start.3 = (bf16[64,256]{1,0:T(8,128)(2,1)S(1)}, bf16[64,256]{1,0:T(8,128)(2,1)S(1)}, u32[]{:S(2)}, u32[]{:S(2)}) collective-permute-start(bf16[64,256]{1,0:T(8,128)(2,1)S(1)} %collective-permute-done.2.refs_2_), channel_id=1, source_target_pairs={{0,2},{1,3},{2,0},{3,1},{4,6},{5,7},{6,4},{7,5},{8,10},{9,11},{10,... | collective-permute-start | bytes 98312 | tf_op jit(solution)/shard_map/ppermute | solution.py:393
  11.7 0.0 collective-permute-done.1.refs_1_
  11.7 1.9 %collective-permute-done.3.refs_3_ = bf16[64,256]{1,0:T(8,128)(2,1)S(1)} collective-permute-done((bf16[64,256]{1,0:T(8,128)(2,1)S(1)}, bf16[64,256]{1,0:T(8,128)(2,1)S(1)}, u32[]{:S(2)}, u32[]{:S(2)}) %collective-permute-start.3) | collective-permute-done | bytes 32800 | tf_op jit(solution)/shard_map/ppermute | solution.py:393
  13.7 0.0 collective-permute-done.recv_ref
  13.7 0.7 %shard_map.39 = (f32[4,64,256]{2,1,0:T(8,128)S(1)}, bf16[4,64,256]{2,1,0:T(8,128)(2,1)S(1)}, f32[64,64]{1,0:T(8,128)S(1)}, s32[144,256]{1,0:T(8,128)S(1)}, s32[1...) custom-call(f32[4,4,64,256]{3,2,1,0:T(8,128)S(1)} %get-tuple-element.21.keep_ref, ...), custom_call_target="tpu_custom_call" | custom-call | flops 1048576 | bytes 2097152 | tf_op jit(solution)/shard_map/pallas_call | solution.py:187
  14.4 2.1 %collective-permute-start.5 = (s32[144,256]{1,0:T(8,128)S(1)}, s32[144,256]{1,0:T(8,128)S(1)}, u32[]{:S(2)}, u32[]{:S(2)}) collective-permute-start(s32[144,256]{1,0:T(8,128)S(1)} %get-tuple-element.26), channel_id=1, source_target_pairs={{0,8},{8,0},{16,24},{24,16},{1,9},{9,1},{17,25},{25,17},{2,10},{10... | collective-permute-start | bytes 442376 | tf_op jit(solution)/shard_map/ppermute | solution.py:399
  16.5 2.2 %collective-permute-start.6 = (s32[144,256]{1,0:T(8,128)S(1)}, s32[144,256]{1,0:T(8,128)S(1)}, u32[]{:S(2)}, u32[]{:S(2)}) collective-permute-start(s32[144,256]{1,0:T(8,128)S(1)} %get-tuple-element.27), channel_id=1, source_target_pairs={{0,16},{8,24},{16,0},{24,8},{1,17},{9,25},{17,1},{25,9},{2,18},{10... | collective-permute-start | bytes 442376 | tf_op jit(solution)/shard_map/ppermute | solution.py:399
  18.6 0.0 collective-permute-start.7
  18.6 2.0 %collective-permute-done.5.refs_0_ = s32[144,256]{1,0:T(8,128)S(1)} collective-permute-done((s32[144,256]{1,0:T(8,128)S(1)}, s32[144,256]{1,0:T(8,128)S(1)}, u32[]{:S(2)}, u32[]{:S(2)}) %collective-permute-start.5) | collective-permute-done | bytes 147488 | tf_op jit(solution)/shard_map/ppermute | solution.py:399
  20.6 2.7 %collective-permute-done.6.refs_1_ = s32[144,256]{1,0:T(8,128)S(1)} collective-permute-done((s32[144,256]{1,0:T(8,128)S(1)}, s32[144,256]{1,0:T(8,128)S(1)}, u32[]{:S(2)}, u32[]{:S(2)}) %collective-permute-start.6) | collective-permute-done | bytes 147488 | tf_op jit(solution)/shard_map/ppermute | solution.py:399
  23.3 1.4 %collective-permute-done.7.refs_2_ = s32[144,256]{1,0:T(8,128)S(1)} collective-permute-done((s32[144,256]{1,0:T(8,128)S(1)}, s32[144,256]{1,0:T(8,128)S(1)}, u32[]{:S(2)}, u32[]{:S(2)}) %collective-permute-start.7) | collective-permute-done | bytes 147488 | tf_op jit(solution)/shard_map/ppermute | solution.py:399
  24.7 0.5 %shard_map.41 = (f32[64,256]{1,0:T(8,128)S(1)}, s32[72,128]{1,0:T(8,128)S(1)}, s32[72,128]{1,0:T(8,128)S(1)}, s32[72,128]{1,0:T(8,128)S(1)}, bf16[13,64,256]{2,1,0:T(8,128)(2,1)S(1)}, /*index=5*/f32[64,64]{1,0:T(8,128)S(1)}) custom-call(f32[4,64,256]{2,1,0:T(8,128)S(1)} %get-tuple-element.24.own_ref, f32[64,64]{1,0:T(8,128)S(1)} %get-tuple-element.25.gram_ref, ...), custom_call_target="tpu_custom_call" | custom-call | flops 524288 | bytes 1048576 | tf_op jit(solution)/shard_map/pallas_call | solution.py:239
  25.2 0.1 collective-permute-start.8
  25.3 0.5 %collective-permute-start.4 = (bf16[4,64,256]{2,1,0:T(8,128)(2,1)S(1)}, bf16[4,64,256]{2,1,0:T(8,128)(2,1)S(1)}, u32[]{:S(2)}, u32[]{:S(2)}) collective-permute-start(bf16[4,64,256]{2,1,0:T(8,128)(2,1)S(1)} %get-tuple-element.23.mine_ref), channel_id=1, source_target_pairs={{0,1},{1,0},{2,3},{3,2},{4,5},{5,4},{6,7},{7,6},{8,9},{9,8},{10,11... | collective-permute-start | bytes 393224 | tf_op jit(solution)/shard_map/ppermute | solution.py:396
  25.8 1.7 %collective-permute-start.9 = (s32[72,128]{1,0:T(8,128)S(1)}, s32[72,128]{1,0:T(8,128)S(1)}, u32[]{:S(2)}, u32[]{:S(2)}) collective-permute-start(s32[72,128]{1,0:T(8,128)S(1)} %get-tuple-element.34), channel_id=1, source_target_pairs={{0,2},{1,3},{2,0},{3,1},{4,6},{5,7},{6,4},{7,5},{8,10},{9,11},{10,... | collective-permute-start | bytes 110600 | tf_op jit(solution)/shard_map/ppermute | solution.py:393
  27.5 3.1 %collective-permute-start.10 = (s32[72,128]{1,0:T(8,128)S(1)}, s32[72,128]{1,0:T(8,128)S(1)}, u32[]{:S(2)}, u32[]{:S(2)}) collective-permute-start(s32[72,128]{1,0:T(8,128)S(1)} %get-tuple-element.35), channel_id=1, source_target_pairs={{0,4},{1,5},{2,6},{3,7},{4,0},{5,1},{6,2},{7,3},{8,12},{9,13},{10,... | collective-permute-start | bytes 110600 | tf_op jit(solution)/shard_map/ppermute | solution.py:393
  30.6 0.0 collective-permute-start.11
  30.6 0.0 collective-permute-done.4.theirs_ref
  30.6 1.1 %shard_map.40.near_ref = f32[256,64]{1,0:T(8,128)S(1)} custom-call(s32[4,10]{1,0:T(4,128)} %bitcast.6, bf16[4,10,256,256]{3,2,1,0:T(8,128)(2,1)S(1)} %bitcast.3, bf16[4,64,256]{2,1,0:T(8,128)(2,1)S(1)} %get-tuple-element.23.mine_ref, bf16[4,64,256]{2,1,0:T(8,128)(2,1)S(1)} %collective-permute-done.4.theirs_ref), custom_call_target="tpu_custom_call" | custom-call | flops 83886080 | bytes 1310720 | tf_op jit(solution)/shard_map/pallas_call | solution.py:279
  31.8 0.0 collective-permute-done.8.refs_1_
  31.8 0.9 %shard_map.42 = (f32[64,256]{1,0:T(8,128)S(1)}, f32[64,64]{1,0:T(8,128)S(1)}) custom-call(s32[4,10]{1,0:T(4,128)} %bitcast.7, bf16[4,10,256,256]{3,2,1,0:T(8,128)(2,1)S(1)} %bitcast.4, bf16[64,256]{1,0:T(8,128)(2,1)S(1)} %copy-done.1, f32[256,64]{1,0:T(8,128)S(1)} %shard_map.40.near_ref, f32[64,64]{1,0:T(8,128)S(1)} %get-tuple-element.29.part_ref, ...), custom_call_target="tpu_custom_call" | custom-call | flops 335544320 | bytes 5242880 | tf_op jit(solution)/shard_map/pallas_call | solution.py:328
  32.7 0.0 collective-permute-done.9.refs_0_
  32.7 0.6 %collective-permute-done.10.refs_1_ = s32[72,128]{1,0:T(8,128)S(1)} collective-permute-done((s32[72,128]{1,0:T(8,128)S(1)}, s32[72,128]{1,0:T(8,128)S(1)}, u32[]{:S(2)}, u32[]{:S(2)}) %collective-permute-start.10) | collective-permute-done | bytes 36896 | tf_op jit(solution)/shard_map/ppermute | solution.py:393
  33.3 3.0 %collective-permute-done.11.refs_2_ = s32[72,128]{1,0:T(8,128)S(1)} collective-permute-done((s32[72,128]{1,0:T(8,128)S(1)}, s32[72,128]{1,0:T(8,128)S(1)}, u32[]{:S(2)}, u32[]{:S(2)}) %collective-permute-start.11) | collective-permute-done | bytes 36896 | tf_op jit(solution)/shard_map/ppermute | solution.py:393
  36.4 1.3 %shard_map.43 = f32[64,256]{1,0:T(8,128)} custom-call(f32[64,256]{1,0:T(8,128)S(1)} %get-tuple-element.31.base_ref, f32[64,64]{1,0:T(8,128)S(1)} %get-tuple-element.32.gram_ref, bf16[64,256]{1,0:T(8,128)(2,1)S(1)} %copy-done.1, f32[64,256]{1,0:T(8,128)S(1)} %get-tuple-element.33.own_ref, s32[72,128]{1,0:T(8,128)S(1)} %collective-permute-done.9.refs_0_, ...), custom_call_target="tpu_custom_call" | custom-call | flops 2097152 | bytes 393216 | tf_op jit(solution)/shard_map/pallas_call | solution.py:375
  (1 shorter events, 0.0 us)
Async XLA Ops:
  0.0 2.5 %copy-start = (bf16[1,4,10,256,256]{4,3,2,1,0:T(8,128)(2,1)S(1)}, bf16[1,4,10,256,256]{4,3,2,1,0:T(8,128)(2,1)}, u32[]{:S(2)}) copy-start(bf16[1,4,10,256,256]{4,3,2,1,0:T(8,128)(2,1)} %param.3) | copy-start | bytes 15728644
  0.0 2.5 %copy-start.1 = (bf16[64,256]{1,0:T(8,128)(2,1)S(1)}, bf16[64,256]{1,0:T(8,128)(2,1)}, u32[]{:S(2)}) copy-start(bf16[64,256]{1,0:T(8,128)(2,1)} %factor_ref.5) | copy-start | bytes 98308
  3.5 10.1 %collective-permute-start = (f32[4,4,64,256]{3,2,1,0:T(8,128)S(1)}, f32[4,4,64,256]{3,2,1,0:T(8,128)S(1)}, u32[]{:S(2)}, u32[]{:S(2)}) collective-permute-start(f32[4,4,64,256]{3,2,1,0:T(8,128)S(1)} %get-tuple-element.22), channel_id=1, source_target_pairs={{0,1},{1,0},{2,3},{3,2},{4,5},{5,4},{6,7},{7,6},{8,9},{9,8},{10,11... | collective-permute-start | bytes 3145736 | tf_op jit(solution)/shard_map/ppermute | solution.py:396
  4.1 5.6 %collective-permute-start.2 = (bf16[64,256]{1,0:T(8,128)(2,1)S(1)}, bf16[64,256]{1,0:T(8,128)(2,1)S(1)}, u32[]{:S(2)}, u32[]{:S(2)}) collective-permute-start(bf16[64,256]{1,0:T(8,128)(2,1)S(1)} %copy-done.1), channel_id=1, source_target_pairs={{0,4},{1,5},{2,6},{3,7},{4,0},{5,1},{6,2},{7,3},{8,12},{9,13},{10,... | collective-permute-start | bytes 98312 | tf_op jit(solution)/shard_map/ppermute | solution.py:393
  7.8 4.0 %collective-permute-start.1 = (bf16[64,256]{1,0:T(8,128)(2,1)S(1)}, bf16[64,256]{1,0:T(8,128)(2,1)S(1)}, u32[]{:S(2)}, u32[]{:S(2)}) collective-permute-start(bf16[64,256]{1,0:T(8,128)(2,1)S(1)} %copy-done.1), channel_id=1, source_target_pairs={{0,2},{1,3},{2,0},{3,1},{4,6},{5,7},{6,4},{7,5},{8,10},{9,11},{10,... | collective-permute-start | bytes 98312 | tf_op jit(solution)/shard_map/ppermute | solution.py:393
  9.7 3.9 %collective-permute-start.3 = (bf16[64,256]{1,0:T(8,128)(2,1)S(1)}, bf16[64,256]{1,0:T(8,128)(2,1)S(1)}, u32[]{:S(2)}, u32[]{:S(2)}) collective-permute-start(bf16[64,256]{1,0:T(8,128)(2,1)S(1)} %collective-permute-done.2.refs_2_), channel_id=1, source_target_pairs={{0,2},{1,3},{2,0},{3,1},{4,6},{5,7},{6,4},{7,5},{8,10},{9,11},{10,... | collective-permute-start | bytes 98312 | tf_op jit(solution)/shard_map/ppermute | solution.py:393
  14.4 6.3 %collective-permute-start.5 = (s32[144,256]{1,0:T(8,128)S(1)}, s32[144,256]{1,0:T(8,128)S(1)}, u32[]{:S(2)}, u32[]{:S(2)}) collective-permute-start(s32[144,256]{1,0:T(8,128)S(1)} %get-tuple-element.26), channel_id=1, source_target_pairs={{0,8},{8,0},{16,24},{24,16},{1,9},{9,1},{17,25},{25,17},{2,10},{10... | collective-permute-start | bytes 442376 | tf_op jit(solution)/shard_map/ppermute | solution.py:399
  16.5 6.8 %collective-permute-start.6 = (s32[144,256]{1,0:T(8,128)S(1)}, s32[144,256]{1,0:T(8,128)S(1)}, u32[]{:S(2)}, u32[]{:S(2)}) collective-permute-start(s32[144,256]{1,0:T(8,128)S(1)} %get-tuple-element.27), channel_id=1, source_target_pairs={{0,16},{8,24},{16,0},{24,8},{1,17},{9,25},{17,1},{25,9},{2,18},{10... | collective-permute-start | bytes 442376 | tf_op jit(solution)/shard_map/ppermute | solution.py:399
  18.6 6.0 %collective-permute-start.7 = (s32[144,256]{1,0:T(8,128)S(1)}, s32[144,256]{1,0:T(8,128)S(1)}, u32[]{:S(2)}, u32[]{:S(2)}) collective-permute-start(s32[144,256]{1,0:T(8,128)S(1)} %get-tuple-element.28), channel_id=1, source_target_pairs={{0,24},{8,16},{16,8},{24,0},{1,25},{9,17},{17,9},{25,1},{2,26},{10... | collective-permute-start | bytes 442376 | tf_op jit(solution)/shard_map/ppermute | solution.py:399
  25.2 6.5 %collective-permute-start.8 = (bf16[13,64,256]{2,1,0:T(8,128)(2,1)S(1)}, bf16[13,64,256]{2,1,0:T(8,128)(2,1)S(1)}, u32[]{:S(2)}, u32[]{:S(2)}) collective-permute-start(bf16[13,64,256]{2,1,0:T(8,128)(2,1)S(1)} %get-tuple-element.30.refs_0_), channel_id=1, source_target_pairs={{0,1},{1,0},{2,3},{3,2},{4,5},{5,4},{6,7},{7,6},{8,9},{9,8},{10,11... | collective-permute-start | bytes 1277960 | tf_op jit(solution)/shard_map/ppermute | solution.py:396
  25.3 5.3 %collective-permute-start.4 = (bf16[4,64,256]{2,1,0:T(8,128)(2,1)S(1)}, bf16[4,64,256]{2,1,0:T(8,128)(2,1)S(1)}, u32[]{:S(2)}, u32[]{:S(2)}) collective-permute-start(bf16[4,64,256]{2,1,0:T(8,128)(2,1)S(1)} %get-tuple-element.23.mine_ref), channel_id=1, source_target_pairs={{0,1},{1,0},{2,3},{3,2},{4,5},{5,4},{6,7},{7,6},{8,9},{9,8},{10,11... | collective-permute-start | bytes 393224 | tf_op jit(solution)/shard_map/ppermute | solution.py:396
  25.8 6.9 %collective-permute-start.9 = (s32[72,128]{1,0:T(8,128)S(1)}, s32[72,128]{1,0:T(8,128)S(1)}, u32[]{:S(2)}, u32[]{:S(2)}) collective-permute-start(s32[72,128]{1,0:T(8,128)S(1)} %get-tuple-element.34), channel_id=1, source_target_pairs={{0,2},{1,3},{2,0},{3,1},{4,6},{5,7},{6,4},{7,5},{8,10},{9,11},{10,... | collective-permute-start | bytes 110600 | tf_op jit(solution)/shard_map/ppermute | solution.py:393
  27.5 5.8 %collective-permute-start.10 = (s32[72,128]{1,0:T(8,128)S(1)}, s32[72,128]{1,0:T(8,128)S(1)}, u32[]{:S(2)}, u32[]{:S(2)}) collective-permute-start(s32[72,128]{1,0:T(8,128)S(1)} %get-tuple-element.35), channel_id=1, source_target_pairs={{0,4},{1,5},{2,6},{3,7},{4,0},{5,1},{6,2},{7,3},{8,12},{9,13},{10,... | collective-permute-start | bytes 110600 | tf_op jit(solution)/shard_map/ppermute | solution.py:393
  30.6 5.8 %collective-permute-start.11 = (s32[72,128]{1,0:T(8,128)S(1)}, s32[72,128]{1,0:T(8,128)S(1)}, u32[]{:S(2)}, u32[]{:S(2)}) collective-permute-start(s32[72,128]{1,0:T(8,128)S(1)} %get-tuple-element.36), channel_id=1, source_target_pairs={{0,6},{1,7},{2,4},{3,5},{4,2},{5,3},{6,0},{7,1},{8,14},{9,15},{10,... | collective-permute-start | bytes 110600 | tf_op jit(solution)/shard_map/ppermute | solution.py:393
